TPU v7x, 128 devices: a whole 4x4x4 slice. The times are simulated.
128 devices in a mesh: teacher: 8 (over z_hi, y), student: 16 (over z_lo, x, core).
Axes of the slice: x: 4, y: 4, z: 4 (z_hi: 2, z_lo: 2; z = z_hi * 2 + z_lo), core: 2. Of those that a mesh axis runs over, the one named last changes fastest.
Arguments:
- teacher_in: bfloat16 [16384, 8192], P('student', 'teacher')
- teacher_attn: bfloat16 [16384, 4096], P('student', 'teacher'), may hold values from -6 to 6
- teacher_out_proj: bfloat16 [4096, 8192], P('student', 'teacher'), may hold values from -0.09375 to 0.09375
- teacher_gain: bfloat16 [8192], P('teacher'), may hold values from 0.099609375 to 1.8984375
- projection: bfloat16 [8192, 4096], P('teacher', 'student'), may hold values from -0.0625 to 0.0625
- student_in: bfloat16 [16384, 4096], P('student', 'teacher')
- student_attn: bfloat16 [16384, 2048], P('student', 'teacher'), may hold values from -6 to 6
- student_out_proj: bfloat16 [2048, 4096], P('student', 'teacher'), may hold values from -0.125 to 0.125
- student_gain: bfloat16 [4096], P('teacher'), may hold values from 0.099609375 to 1.8984375
- token_ids: int32 [16384], P('student'), may hold values from 0 to 128004, as said below
- row_order: int32 [16384], replicated, may hold values from 0 to 16383, as said below
Outputs:
- grad_weight: float32 [2048, 4096], P('student', 'teacher')
- grad_gain: float32 [4096], P('teacher')
Inputs may be any that keep to these rules, and one draw needn't show every extreme that they name: `token_ids`: within each sequence of 1024 consecutive rows the rows holding 128004 form the sequence's tail, after at least 256 other rows; no other row holds 128004. `row_order`: A permutation of the 16384 rows. For student block k and teacher block b (blocks of 1024 rows), the entries k * 1024 + b * 64 to k * 1024 + (b + 1) * 64 - 1 name rows of teacher block b.
All inputs are finite; a program needn't handle non-finite values.
Results may differ from a plain program's by a relative error of at most 0.02.
Values may be sent and summed in bfloat16 or wider, within the bound.
A program may use at most 128 MiB of HBM per device.

v0:
```python
import math
import jax
import jax.numpy as jnp
from jax import lax
from jax.sharding import PartitionSpec as P

DT = 8192
DS = 4096
PAD_ID = 128004
epsilon = 1e-05


def rows_first(arrays, axis, dims):
    turned = [jnp.moveaxis(a, dim, 0) for a, dim in zip(arrays, dims)]
    both = jnp.concatenate([t.reshape(len(t), -1) for t in turned], axis=1)
    result, at, outs = (lax.all_gather(both, axis, axis=0, tiled=True), 0, [])
    for t, dim in zip(turned, dims):
        section = result[:, at : at + t[0].size].reshape(-1, *t.shape[1:])
        outs.append(jnp.moveaxis(section, 0, dim))
        at += t[0].size
    return tuple(outs)


def sent_to_all(array, axis):
    peers = lax.axis_size(axis)
    return lax.all_to_all(
        jnp.broadcast_to(array[None], (peers, *array.shape)), axis, 0, 0, tiled=True
    )


def of_everyone(array, axis):
    everything = sent_to_all(array, axis)
    return jnp.sum(everything, axis=0)


def sent_together(arrays, axis, split_dim, concat_dim, along):
    columns = [a.reshape(*a.shape[:along], -1) for a in arrays]
    both = jnp.concatenate(columns, axis=along)
    result, at, outs = (
        lax.all_to_all(both, axis, split_axis=split_dim, concat_axis=concat_dim, tiled=True),
        0,
        [],
    )
    for a, column in zip(arrays, columns):
        section = result[..., at : at + column.shape[along]]
        outs.append(section.reshape(*section.shape[:along], *a.shape[along:]))
        at += column.shape[along]
    return tuple(outs)


def in_blocks(array, dim, peers):
    shape = array.shape
    parts = array.reshape(*shape[:dim], peers, shape[dim] // peers, *shape[dim + 1 :])
    return jnp.moveaxis(parts, dim, 0)


def sent_and_summed(array, axis, dim):
    peers = lax.axis_size(axis)
    parts = lax.all_to_all(in_blocks(array, dim, peers), axis, 0, 0, tiled=True)
    return jnp.sum(parts.astype(jnp.float32), axis=0)


def shards(
    teacher_in,
    teacher_attn,
    teacher_out_proj,
    teacher_gain,
    projection,
    student_in,
    student_attn,
    student_out_proj,
    student_gain,
    token_ids,
    row_order,
):
    student_count = lax.axis_size("student")
    teacher_count = lax.axis_size("teacher")
    row_count = teacher_in.shape[0]
    piece_rows = row_count // student_count
    student_index = lax.axis_index("student")
    attn_all = lax.all_gather(teacher_attn, "teacher", axis=1, tiled=True)
    out_full, proj_full = rows_first((teacher_out_proj, projection), "student", (0, 1))
    branch = jnp.dot(attn_all, out_full, preferred_element_type=jnp.float32)
    residual = teacher_in.astype(jnp.float32) + branch
    square_sum = of_everyone(jnp.sum(residual * residual, axis=1), "teacher")
    teacher_scale = lax.rsqrt(square_sum / DT + epsilon)
    hidden = (residual * teacher_scale[:, None] * teacher_gain.astype(jnp.float32)[None, :]).astype(
        jnp.bfloat16
    )
    proj_blocks = proj_full.reshape(
        proj_full.shape[0], teacher_count, proj_full.shape[1] // teacher_count
    )
    row_blocks = row_order.reshape(student_count, student_count, piece_rows)
    local_rows = (
        lax.dynamic_index_in_dim(row_blocks, student_index, 1, keepdims=False)
        - student_index * row_count
    )
    live_rows = jnp.where(token_ids != PAD_ID, 1.0, 0.0).astype(jnp.bfloat16)
    mask_send = jnp.take(live_rows, local_rows, axis=0)
    columns = proj_blocks
    summed = lax.psum_scatter(
        jnp.einsum("tf,fko->kto", hidden, columns, preferred_element_type=jnp.float32).astype(
            jnp.bfloat16
        ),
        "teacher",
        scatter_dimension=0,
        tiled=True,
    ).astype(jnp.float32)
    target_rows = summed[0].astype(jnp.bfloat16)
    moved, mask_got = sent_together(
        (jnp.take(target_rows, local_rows, axis=0), mask_send), "student", 0, 0, 2
    )
    target = moved.reshape(row_count, moved.shape[2])
    weight_mask = mask_got.reshape(row_count).astype(jnp.float32)
    attn_student = lax.all_gather(student_attn, "teacher", axis=1, tiled=True)
    columns = attn_student
    student_branch = jnp.dot(
        columns,
        lax.all_gather(student_out_proj, "student", axis=0, tiled=True),
        preferred_element_type=jnp.float32,
    )
    student_res = student_in.astype(jnp.float32) + student_branch
    student_square = of_everyone(jnp.sum(student_res * student_res, axis=1), "teacher")
    student_scale = lax.rsqrt(student_square / DS + epsilon)
    normed = student_res * student_scale[:, None]
    gain_values = student_gain.astype(jnp.float32)[None, :]
    distance = normed * gain_values - target.astype(jnp.float32)
    loss_weight = 1.0 / math.sqrt(row_count * student_count)
    grad_out = distance * (weight_mask * loss_weight)[:, None]
    gain_part = jnp.sum(grad_out * normed, axis=0)
    grad_norm = grad_out * gain_values
    inner_sum = of_everyone(jnp.sum(grad_norm * normed, axis=1), "teacher")
    grad_res = (student_scale[:, None] * (grad_norm - normed * (inner_sum / DS)[:, None])).astype(
        jnp.bfloat16
    )
    columns = attn_student
    grad_weight = sent_and_summed(
        lax.dot_general(
            columns, grad_res, (((0,), (0,)), ((), ())), preferred_element_type=jnp.float32
        ).astype(jnp.bfloat16),
        "student",
        0,
    )
    grad_gain = of_everyone(gain_part, "student")
    return (grad_weight, grad_gain)


def solution(mesh):
    placed = (
        P("student", "teacher"),
        P("student", "teacher"),
        P("student", "teacher"),
        P("teacher"),
        P("teacher", "student"),
        P("student", "teacher"),
        P("student", "teacher"),
        P("student", "teacher"),
        P("teacher"),
        P("student"),
        P(),
    )
    return jax.shard_map(
        shards,
        mesh=mesh,
        in_specs=placed,
        out_specs=(P("student", "teacher"), P("teacher")),
        check_vma=False,
    )
```

profile of v0, /device:TPU:3, one launch (start us, length us, event | category | flops | bytes accessed | tf_op | source)
XLA Modules:
  0.0 564.8 jit_solution(5684495137640013331)
XLA Ops:
  7.2 0.7 all-gather.11.cloned.1.call-update
  8.0 1.2 copy.60
  9.2 1.1 pad_maximum_fusion.1
  11.7 2.6 copy.62
  14.3 116.5 %all-gather.11.cloned.1.call-done = bf16[1024,4096]{1,0:T(8,128)(2,1)} async-done(((bf16[1024,512]{1,0:T(8,128)(2,1)}), bf16[1024,4096]{1,0:T(8,128)(2,1)}) %all-gather.11.cloned.1.call-update) | async-done | bytes 8388624 | tf_op jit(solution)/shard_map/all_gather | solution.py:81
  130.8 99.5 %all-gather.9.cloned.1.call-done = bf16[4096,2048]{0,1:T(8,128)(2,1)} async-done(((bf16[256,2048]{0,1:T(8,128)(2,1)}), bf16[4096,2048]{0,1:T(8,128)(2,1)}) %all-gather.9.cloned.1.call-update) | async-done | bytes 16777232 | tf_op jit(solution)/shard_map/all_gather | solution.py:16
  230.3 15.4 %multiply_reduce_fusion = (f32[1024]{0:T(1024)S(1)}, f32[1024,1024]{1,0:T(8,128)}) fusion(bf16[1024,1024]{0,1:T(8,128)(2,1)} %copy.62, bf16[1024,4096]{1,0:T(8,128)(2,1)} %all-gather.11.cloned.1.call-done, bf16[4096,2048]{0,1:T(8,128)(2,1)} %all-gather.9.cloned.1.call-done), kind=kOutput, calls=%fused_computation.9 | convolution fusion | flops 8594127872 | bytes 23072768 | tf_op jit(solution)/shard_map/dot_general | solution.py:83
  246.4 6.3 %all-to-all-start.1 = ((f32[8,1,1024]{2,1,0:T(1,128)}), f32[8,1,1024]{2,1,0:T(1,128)S(1)}, u32[]{:S(2)}, u32[]{:S(2)}) async-start(f32[8,1,1024]{2,1,0:T(1,128)} %broadcast_in_dim.34), calls=%async_computation.1 | async-start | bytes 65536 | tf_op jit(solution)/shard_map/all_to_all | solution.py:26
  252.9 7.8 %slice_bitcast_fusion = bf16[1024,4096]{1,0:T(8,128)(2,1)} fusion(bf16[4096,2048]{0,1:T(8,128)(2,1)} %all-gather.9.cloned.1.call-done), kind=kLoop, calls=%fused_computation.4 | loop fusion | bytes 16777216 | tf_op jit(solution)/shard_map/transpose | solution.py:19
  260.7 12.1 %copy.61 = bf16[1024,4096]{0,1:T(8,128)(2,1)} copy(bf16[1024,4096]{1,0:T(8,128)(2,1)} %slice_bitcast_fusion) | data formatting | bytes 16777216 | tf_op jit(solution)/shard_map/transpose | solution.py:19
  272.9 15.4 %convert_bitcast_fusion = bf16[8,1024,512]{1,2,0:T(8,128)(2,1)} fusion(bf16[1024,8,512]{0,2,1:T(8,128)(2,1)} %bitcast.38, f32[1024,1024]{1,0:T(8,128)} %get-tuple-element.11, bf16[1024,1024]{0,1:T(8,128)(2,1)S(1)} %copy-done.1, f32[1024]{0:T(1024)S(1)} %convert_element_type.58, f32[1024]{0:T(1024)S(1)} %add_rsqrt_fusion), kind=kOutput, calls=%fused_computation.5 | convolution fusion | flops 8599371776 | bytes 23076864 | tf_op jit(solution)/shard_map/tf,fko->kto/dot_general | solution.py:102
  288.4 0.8 copy-done.4
  289.4 6.8 %gather_fusion.1 = bf16[1024]{0:T(1024)(128)(2,1)S(1)} fusion(bf16[1024]{0:T(1024)(128)(2,1)S(1)} %select_convert_fusion, s32[1024]{0:T(1024)S(1)} %broadcast_clamp_fusion), kind=kCustom, calls=%fused_computation.1 | custom fusion | bytes 8192 | tf_op jit(solution)/shard_map/jit(_take)/gather | solution.py:99
  297.1 46.7 %all-gather.5.cloned.1.call-done = bf16[1024,2048]{1,0:T(8,128)(2,1)} async-done(((bf16[1024,256]{1,0:T(8,128)(2,1)}), bf16[1024,2048]{1,0:T(8,128)(2,1)}) %all-gather.5.cloned.1.call-update) | async-done | bytes 4194320 | tf_op jit(solution)/shard_map/all_gather | solution.py:115
  343.9 6.6 %multiply_reduce_fusion.3 = (f32[1024]{0:T(1024)S(1)}, f32[1024,512]{0,1:T(8,128)}) fusion(bf16[1024,2048]{1,0:T(8,128)(2,1)} %all-gather.5.cloned.1.call-done, bf16[2048,512]{1,0:T(8,128)(2,1)} %all-gather.7.cloned.1.call-done, bf16[1024,512]{0,1:T(8,128)(2,1)S(1)} %copy.58), kind=kOutput, calls=%fused_computation.19 | convolution fusion | flops 2149579776 | bytes 9441280 | tf_op jit(solution)/shard_map/dot_general | solution.py:117
  351.1 3.4 all-to-all-start
  354.5 107.1 %reduce-scatter.2.cloned.1.call-done = bf16[1,1024,512]{1,2,0:T(8,128)(2,1)} async-done(((bf16[8,1024,512]{1,2,0:T(8,128)(2,1)}), bf16[1,1024,512]{1,2,0:T(8,128)(2,1)}) %reduce-scatter.2.cloned.1.call-update) | async-done | bytes 1048592 | tf_op jit(solution)/shard_map/reduce_scatter | solution.py:101
  461.6 1.5 copy.65
  463.1 4.0 gather_fusion
  467.3 1.2 pad_maximum_fusion
  468.4 5.9 %all-to-all-start.2 = ((bf16[16,64,513]{2,1,0:T(8,128)(2,1)}), bf16[16,64,513]{2,1,0:T(8,128)(2,1)S(1)}, u32[]{:S(2)}, u32[]{:S(2)}) async-start(bf16[16,64,513]{2,1,0:T(8,128)(2,1)} %pad_maximum_fusion), calls=%async_computation.3 | async-start | bytes 2621440 | tf_op jit(solution)/shard_map/all_to_all | solution.py:40
  474.5 16.8 %all-to-all-done.2 = bf16[16,64,513]{2,1,0:T(8,128)(2,1)S(1)} async-done(((bf16[16,64,513]{2,1,0:T(8,128)(2,1)}), bf16[16,64,513]{2,1,0:T(8,128)(2,1)S(1)}, u32[]{:S(2)}, u32[]{:S(2)}) %all-to-all-start.2) | async-done | bytes 1050656 | tf_op jit(solution)/shard_map/all_to_all | solution.py:40
  491.3 1.7 bitcast_convert_fusion
  493.0 1.9 copy.67
  495.2 2.4 multiply_reduce_fusion.1
  497.6 10.2 %all_to_all.34 = f32[8,1,1024]{2,1,0:T(1,128)S(1)} all-to-all(f32[8,1,1024]{2,1,0:T(1,128)S(1)} %broadcast_in_dim.62), channel_id=1, replica_groups=mesh['teacher'=8,'student'=16] {'teacher'}, dimensions={0} | all-to-all | bytes 65536 | tf_op jit(solution)/shard_map/all_to_all | solution.py:26
  508.4 7.2 %all-to-all-start.5 = ((f32[16,1,512]{2,1,0:T(1,128)}), f32[16,1,512]{2,1,0:T(1,128)S(1)}, u32[]{:S(2)}, u32[]{:S(2)}) async-start(f32[16,1,512]{2,1,0:T(1,128)} %broadcast_in_dim.63), calls=%async_computation.6 | async-start | bytes 65536 | tf_op jit(solution)/shard_map/all_to_all | solution.py:26
  515.7 5.4 fusion.6
  521.1 1.9 copy.82
  523.0 5.8 %all-to-all-start.4 = ((bf16[16,128,512]{1,2,0:T(8,128)(2,1)}), bf16[16,128,512]{1,2,0:T(8,128)(2,1)S(1)}, u32[]{:S(2)}, u32[]{:S(2)}) async-start(bf16[16,128,512]{1,2,0:T(8,128)(2,1)} %bitcast.37), calls=%async_computation.5 | async-start | bytes 4194304 | tf_op jit(solution)/shard_map/all_to_all | solution.py:59
  529.4 27.7 %all-to-all-done.4 = bf16[16,128,512]{1,2,0:T(8,128)(2,1)S(1)} async-done(((bf16[16,128,512]{1,2,0:T(8,128)(2,1)}), bf16[16,128,512]{1,2,0:T(8,128)(2,1)S(1)}, u32[]{:S(2)}, u32[]{:S(2)}) %all-to-all-start.4) | async-done | bytes 2097184 | tf_op jit(solution)/shard_map/all_to_all | solution.py:59
  557.4 0.8 copy.72
  (57 shorter events, 6.2 us)
Async XLA Ops:
  7.2 2.1 copy-start.3
  7.2 123.6 %all-gather.11.cloned.1.call-start = ((), (), s32[]{:S(2)}) async-start(), calls=%async_computation.10 | async-start | bytes 9437184 | tf_op jit(solution)/shard_map/all_gather | solution.py:81
  7.9 222.4 %all-gather.9.cloned.1.call-start = ((), (), s32[]{:S(2)}) async-start(), calls=%async_computation.9 | async-start | bytes 17825792 | tf_op jit(solution)/shard_map/all_gather | solution.py:16
  9.2 2.5 copy-start
  10.4 286.8 %all-gather.7.cloned.1.call-start = ((), (), s32[]{:S(2)}) async-start(), calls=%async_computation.8 | async-start | bytes 2228224 | tf_op jit(solution)/shard_map/all_gather | solution.py:119
  11.1 332.8 %all-gather.5.cloned.1.call-start = ((), (), s32[]{:S(2)}) async-start(), calls=%async_computation.7 | async-start | bytes 4718592 | tf_op jit(solution)/shard_map/all_gather | solution.py:115
  11.7 2.6 copy-start.6
  246.4 26.5 %all-to-all-start.1 = ((f32[8,1,1024]{2,1,0:T(1,128)}), f32[8,1,1024]{2,1,0:T(1,128)S(1)}, u32[]{:S(2)}, u32[]{:S(2)}) async-start(f32[8,1,1024]{2,1,0:T(1,128)} %broadcast_in_dim.34), calls=%async_computation.1 | async-start | bytes 65536 | tf_op jit(solution)/shard_map/all_to_all | solution.py:26
  252.7 208.9 %reduce-scatter.2.cloned.1.call-start = ((), (), s32[]{:S(2)}) async-start(), calls=%async_computation.11 | async-start | bytes 9437184 | tf_op jit(solution)/shard_map/reduce_scatter | solution.py:101
  260.7 12.2 %copy-start.1 = (bf16[1024,1024]{0,1:T(8,128)(2,1)S(1)}, bf16[1024,1024]{0,1:T(8,128)(2,1)}, u32[]{:S(2)}) copy-start(bf16[1024,1024]{0,1:T(8,128)(2,1)} %copy.62) | copy-start | bytes 6291460
  288.4 0.8 copy-start.4
  288.4 1.0 copy-start.5
  289.4 7.1 %copy-start.2 = (bf16[1024,512]{1,0:T(8,128)(2,1)S(1)}, bf16[1024,512]{1,0:T(8,128)(2,1)}, u32[]{:S(2)}) copy-start(bf16[1024,512]{1,0:T(8,128)(2,1)} %param.16) | copy-start | bytes 3145732
  351.1 117.4 %all-to-all-start = ((f32[8,1,1024]{2,1,0:T(1,128)}), f32[8,1,1024]{2,1,0:T(1,128)S(1)}, u32[]{:S(2)}, u32[]{:S(2)}) async-start(f32[8,1,1024]{2,1,0:T(1,128)} %broadcast_in_dim.32), calls=%async_computation | async-start | bytes 65536 | tf_op jit(solution)/shard_map/all_to_all | solution.py:26
  467.2 7.2 %copy-start.7 = (bf16[512]{0:T(512)(128)(2,1)S(1)}, bf16[512]{0:T(512)(128)(2,1)}, u32[]{:S(2)}) copy-start(bf16[512]{0:T(512)(128)(2,1)} %param.19) | copy-start | bytes 3076
  468.4 22.8 %all-to-all-start.2 = ((bf16[16,64,513]{2,1,0:T(8,128)(2,1)}), bf16[16,64,513]{2,1,0:T(8,128)(2,1)S(1)}, u32[]{:S(2)}, u32[]{:S(2)}) async-start(bf16[16,64,513]{2,1,0:T(8,128)(2,1)} %pad_maximum_fusion), calls=%async_computation.3 | async-start | bytes 2621440 | tf_op jit(solution)/shard_map/all_to_all | solution.py:40
  508.4 14.5 %all-to-all-start.5 = ((f32[16,1,512]{2,1,0:T(1,128)}), f32[16,1,512]{2,1,0:T(1,128)S(1)}, u32[]{:S(2)}, u32[]{:S(2)}) async-start(f32[16,1,512]{2,1,0:T(1,128)} %broadcast_in_dim.63), calls=%async_computation.6 | async-start | bytes 65536 | tf_op jit(solution)/shard_map/all_to_all | solution.py:26
  523.0 34.1 %all-to-all-start.4 = ((bf16[16,128,512]{1,2,0:T(8,128)(2,1)}), bf16[16,128,512]{1,2,0:T(8,128)(2,1)S(1)}, u32[]{:S(2)}, u32[]{:S(2)}) async-start(bf16[16,128,512]{1,2,0:T(8,128)(2,1)} %bitcast.37), calls=%async_computation.5 | async-start | bytes 4194304 | tf_op jit(solution)/shard_map/all_to_all | solution.py:59
Sparse Core Ops, SparseCore 0:
  10.2 120.5 all-gather.10
  132.4 97.8 all-gather.8
  232.0 33.8 all-gather.6
  267.9 75.8 all-gather.4
  347.6 113.9 reduce-scatter.1
where the time goes:
time: 566 us; the launch traced here: 565 us
  waiting for transfers between devices  416 us (73%)
  local copies, waits for them, and re-layouts  44.6 us (8%)
  matrix products  42.8 us (8%)
  starting transfers between devices  29.1 us (5%)
  between operations  14 us (2%)
  blocking collectives  10.2 us (2%)
  other arithmetic  7.84 us (1%)
    all_gather x1, waiting for transfers between devices, shards(): attn_all = lax.all_gather(teacher_attn, 'teacher', axis=1, tiled=True)  117 us
    reduce_scatter x1, waiting for transfers between devices, shards(): lax.psum_scatter(jnp.einsum('tf,fko->kto', hidden, columns, preferred_ele...  107 us
    all_gather x1, waiting for transfers between devices, rows_first(): result, at, outs = (lax.all_gather(both, axis, axis=0, tiled=True), 0, [])  99.5 us
    all_gather x1, waiting for transfers between devices, shards(): attn_student = lax.all_gather(student_attn, 'teacher', axis=1, tiled=True)  46.7 us
    all_to_all x1, waiting for transfers between devices, sent_and_summed(): parts = lax.all_to_all(in_blocks(array, dim, peers), axis, 0, 0, tiled=True)  27.7 us
    transpose x2, local copies, waits for them, and re-layouts, rows_first(): outs.append(jnp.moveaxis(section, 0, dim))  20 us
    all_to_all x3, starting transfers between devices, sent_to_all(): lax.all_to_all(jnp.broadcast_to(array[None], (peers, *array.shape)), axis...  17 us
    all_to_all x1, waiting for transfers between devices, sent_together(): lax.all_to_all(both, axis, split_axis=split_dim, concat_axis=concat_dim,...  16.8 us
  transfers between devices with their start and end apart: 10, of which 6 were waited for; matrix products, arithmetic and copies ran while one was open for 15% of the time, Pallas kernels for 0%

commit v1 on v0

--- a/solution.py
+++ b/solution.py
@@ -1,3 +1,4 @@
+import functools
 import math
 import jax
 import jax.numpy as jnp
@@ -8,6 +9,19 @@
 DS = 4096
 PAD_ID = 128004
 epsilon = 1e-05
+
+
+def _raise_node(view, mesh_dim, at_axis):
+    pool = []
+    for _ in range(lax.axis_size(mesh_dim)):
+        pool.append(view)
+    local_out = jnp.stack(pool)
+    return jnp.concatenate(
+        lax.all_to_all(local_out, split_axis=0, concat_axis=0, axis_name=mesh_dim), at_axis
+    )
+
+
+words_play = functools.partial(_raise_node, mesh_dim="teacher", at_axis=1)
 
 
 def rows_first(arrays, axis, dims):
@@ -112,7 +126,7 @@
     )
     target = moved.reshape(row_count, moved.shape[2])
     weight_mask = mask_got.reshape(row_count).astype(jnp.float32)
-    attn_student = lax.all_gather(student_attn, "teacher", axis=1, tiled=True)
+    attn_student = words_play(student_attn)
     columns = attn_student
     student_branch = jnp.dot(
         columns,

time: 566 us -> 560 us (0.989)
  waiting for transfers between devices: 416 us -> 391 us
  starting transfers between devices: 29.1 us -> 45.6 us
    all_to_all x0 -> x1, waiting for transfers between devices: none -> 57.9 us  [_raise_node(): lax.all_to_all(local_out, split_axis=0, concat_axis=0, axis_name=mesh_dim)]
    all_gather x1 -> x0, waiting for transfers between devices: 46.7 us -> none  [shards(): attn_student = lax.all_gather(student_attn, 'teacher', axis=1, tiled=True)]
    reduce_scatter x1, waiting for transfers between devices: 107 us -> 71.1 us  [shards(): lax.psum_scatter(jnp.einsum('tf,fko->kto', hidden, columns, preferred_ele...]
    all_to_all x3, starting transfers between devices: 17 us -> 27 us  [sent_to_all(): lax.all_to_all(jnp.broadcast_to(array[None], (peers, *array.shape)), axis...]
    all_to_all x0 -> x1, starting transfers between devices: none -> 6.74 us  [_raise_node(): lax.all_to_all(local_out, split_axis=0, concat_axis=0, axis_name=mesh_dim)]
  transfers between devices with their start and end apart: 10 -> 10, of which waited for: 6 -> 6; matrix products, arithmetic and copies ran while one was open for 15% -> 16% of each run, Pallas kernels for 0% -> 0%
where the time goes in v1:
time: 560 us; the launch traced here: 559 us
  waiting for transfers between devices  391 us (70%)
  local copies, waits for them, and re-layouts  47.6 us (8%)
  starting transfers between devices  45.6 us (8%)
  matrix products  42.7 us (8%)
  between operations  14 us (2%)
  blocking collectives  10.2 us (2%)
  other arithmetic  7.85 us (1%)
    all_gather x1, waiting for transfers between devices, shards(): attn_all = lax.all_gather(teacher_attn, 'teacher', axis=1, tiled=True)  117 us
    all_gather x1, waiting for transfers between devices, rows_first(): result, at, outs = (lax.all_gather(both, axis, axis=0, tiled=True), 0, [])  99.5 us
    reduce_scatter x1, waiting for transfers between devices, shards(): lax.psum_scatter(jnp.einsum('tf,fko->kto', hidden, columns, preferred_ele...  71.1 us
    all_to_all x1, waiting for transfers between devices, _raise_node(): lax.all_to_all(local_out, split_axis=0, concat_axis=0, axis_name=mesh_dim)  57.9 us
    all_to_all x1, waiting for transfers between devices, sent_and_summed(): parts = lax.all_to_all(in_blocks(array, dim, peers), axis, 0, 0, tiled=True)  27.7 us
    all_to_all x3, starting transfers between devices, sent_to_all(): lax.all_to_all(jnp.broadcast_to(array[None], (peers, *array.shape)), axis...  27 us
    transpose x2, local copies, waits for them, and re-layouts, rows_first(): outs.append(jnp.moveaxis(section, 0, dim))  19.9 us
    all_to_all x1, waiting for transfers between devices, sent_together(): lax.all_to_all(both, axis, split_axis=split_dim, concat_axis=concat_dim,...  16.8 us
  transfers between devices with their start and end apart: 10, of which 6 were waited for; matrix products, arithmetic and copies ran while one was open for 16% of the time, Pallas kernels for 0%

profile of v1, /device:TPU:3, one launch (start us, length us, event | category | flops | bytes accessed | tf_op | source)
XLA Modules:
  0.0 559.3 jit_solution(820895618791627433)
XLA Ops:
  8.0 1.4 copy.65
  9.4 1.1 pad_maximum_fusion.1
  11.3 2.6 copy.67
  13.8 117.0 %all-gather.8.cloned.1.call-done = bf16[1024,4096]{1,0:T(8,128)(2,1)} async-done(((bf16[1024,512]{1,0:T(8,128)(2,1)}), bf16[1024,4096]{1,0:T(8,128)(2,1)}) %all-gather.8.cloned.1.call-update) | async-done | bytes 8388624 | tf_op jit(solution)/shard_map/all_gather | solution.py:95
  130.8 99.5 %all-gather.6.cloned.1.call-done = bf16[4096,2048]{0,1:T(8,128)(2,1)} async-done(((bf16[256,2048]{0,1:T(8,128)(2,1)}), bf16[4096,2048]{0,1:T(8,128)(2,1)}) %all-gather.6.cloned.1.call-update) | async-done | bytes 16777232 | tf_op jit(solution)/shard_map/all_gather | solution.py:30
  230.3 15.4 %multiply_reduce_fusion = (f32[1024]{0:T(1024)S(1)}, f32[1024,1024]{1,0:T(8,128)}) fusion(bf16[1024,1024]{0,1:T(8,128)(2,1)} %copy.67, bf16[1024,4096]{1,0:T(8,128)(2,1)} %all-gather.8.cloned.1.call-done, bf16[4096,2048]{0,1:T(8,128)(2,1)} %all-gather.6.cloned.1.call-done), kind=kOutput, calls=%fused_computation.9 | convolution fusion | flops 8594127872 | bytes 23072768 | tf_op jit(solution)/shard_map/dot_general | solution.py:97
  246.4 6.3 %all-to-all-start.2 = ((f32[8,1,1024]{2,1,0:T(1,128)}), f32[8,1,1024]{2,1,0:T(1,128)S(1)}, u32[]{:S(2)}, u32[]{:S(2)}) async-start(f32[8,1,1024]{2,1,0:T(1,128)} %broadcast_in_dim.34), calls=%async_computation.2 | async-start | bytes 65536 | tf_op jit(solution)/shard_map/all_to_all | solution.py:40
  252.7 7.8 %slice_bitcast_fusion = bf16[1024,4096]{1,0:T(8,128)(2,1)} fusion(bf16[4096,2048]{0,1:T(8,128)(2,1)} %all-gather.6.cloned.1.call-done), kind=kLoop, calls=%fused_computation.4 | loop fusion | bytes 16777216 | tf_op jit(solution)/shard_map/transpose | solution.py:33
  260.5 12.1 %copy.66 = bf16[1024,4096]{0,1:T(8,128)(2,1)} copy(bf16[1024,4096]{1,0:T(8,128)(2,1)} %slice_bitcast_fusion) | data formatting | bytes 16777216 | tf_op jit(solution)/shard_map/transpose | solution.py:33
  272.7 15.4 %convert_bitcast_fusion = bf16[8,1024,512]{1,2,0:T(8,128)(2,1)} fusion(bf16[1024,8,512]{0,2,1:T(8,128)(2,1)} %bitcast.41, f32[1024,1024]{1,0:T(8,128)} %get-tuple-element.11, bf16[1024,1024]{0,1:T(8,128)(2,1)S(1)} %copy-done.1, f32[1024]{0:T(1024)S(1)} %convert_element_type.58, f32[1024]{0:T(1024)S(1)} %add_rsqrt_fusion), kind=kOutput, calls=%fused_computation.5 | convolution fusion | flops 8599371776 | bytes 23076864 | tf_op jit(solution)/shard_map/tf,fko->kto/dot_general | solution.py:116
  288.1 1.0 copy-done.3
  289.4 2.5 stack.2
  291.8 6.7 %all-to-all-start = ((bf16[8,1024,256]{1,2,0:T(8,128)(2,1)}), bf16[8,1024,256]{1,2,0:T(8,128)(2,1)}, u32[]{:S(2)}, u32[]{:S(2)}) async-start(bf16[8,1024,256]{1,2,0:T(8,128)(2,1)} %stack.2), calls=%async_computation | async-start | bytes 8388608 | tf_op jit(solution)/shard_map/all_to_all | solution.py:20
  298.8 6.8 %gather_fusion.1 = bf16[1024]{0:T(1024)(128)(2,1)S(1)} fusion(bf16[1024]{0:T(1024)(128)(2,1)S(1)} %select_convert_fusion, s32[1024]{0:T(1024)S(1)} %broadcast_clamp_fusion), kind=kCustom, calls=%fused_computation.1 | custom fusion | bytes 8192 | tf_op jit(solution)/shard_map/jit(_take)/gather | solution.py:113
  306.5 57.9 %all-to-all-done = bf16[8,1024,256]{1,2,0:T(8,128)(2,1)} async-done(((bf16[8,1024,256]{1,2,0:T(8,128)(2,1)}), bf16[8,1024,256]{1,2,0:T(8,128)(2,1)}, u32[]{:S(2)}, u32[]{:S(2)}) %all-to-all-start) | async-done | bytes 4194336 | tf_op jit(solution)/shard_map/all_to_all | solution.py:20
  364.4 6.6 %multiply_reduce_fusion.3 = (f32[1024]{0:T(1024)S(1)}, f32[1024,512]{0,1:T(8,128)}) fusion(bf16[1024,2048]{0,1:T(8,128)(2,1)} %bitcast.1, bf16[2048,512]{1,0:T(8,128)(2,1)} %all-gather.4.cloned.1.call-done, bf16[1024,512]{0,1:T(8,128)(2,1)S(1)} %copy.62), kind=kOutput, calls=%fused_computation.19 | convolution fusion | flops 2149579776 | bytes 9441280 | tf_op jit(solution)/shard_map/dot_general | solution.py:131
  371.6 13.5 %all-to-all-start.1 = ((f32[8,1,1024]{2,1,0:T(1,128)}), f32[8,1,1024]{2,1,0:T(1,128)S(1)}, u32[]{:S(2)}, u32[]{:S(2)}) async-start(f32[8,1,1024]{2,1,0:T(1,128)} %broadcast_in_dim.32), calls=%async_computation.1 | async-start | bytes 65536 | tf_op jit(solution)/shard_map/all_to_all | solution.py:40
  385.1 71.1 %reduce-scatter.2.cloned.1.call-done = bf16[1,1024,512]{1,2,0:T(8,128)(2,1)} async-done(((bf16[8,1024,512]{1,2,0:T(8,128)(2,1)}), bf16[1,1024,512]{1,2,0:T(8,128)(2,1)}) %reduce-scatter.2.cloned.1.call-update) | async-done | bytes 1048592 | tf_op jit(solution)/shard_map/reduce_scatter | solution.py:115
  456.1 1.5 copy.70
  457.6 4.0 gather_fusion
  461.8 1.2 pad_maximum_fusion
  463.0 5.9 %all-to-all-start.3 = ((bf16[16,64,513]{2,1,0:T(8,128)(2,1)}), bf16[16,64,513]{2,1,0:T(8,128)(2,1)S(1)}, u32[]{:S(2)}, u32[]{:S(2)}) async-start(bf16[16,64,513]{2,1,0:T(8,128)(2,1)} %pad_maximum_fusion), calls=%async_computation.4 | async-start | bytes 2621440 | tf_op jit(solution)/shard_map/all_to_all | solution.py:54
  469.0 16.8 %all-to-all-done.3 = bf16[16,64,513]{2,1,0:T(8,128)(2,1)S(1)} async-done(((bf16[16,64,513]{2,1,0:T(8,128)(2,1)}), bf16[16,64,513]{2,1,0:T(8,128)(2,1)S(1)}, u32[]{:S(2)}, u32[]{:S(2)}) %all-to-all-start.3) | async-done | bytes 1050656 | tf_op jit(solution)/shard_map/all_to_all | solution.py:54
  485.9 1.7 bitcast_convert_fusion
  487.6 1.9 copy.72
  489.8 2.4 multiply_reduce_fusion.1
  492.2 10.2 %all_to_all.39 = f32[8,1,1024]{2,1,0:T(1,128)S(1)} all-to-all(f32[8,1,1024]{2,1,0:T(1,128)S(1)} %broadcast_in_dim.62), channel_id=1, replica_groups=mesh['teacher'=8,'student'=16] {'teacher'}, dimensions={0} | all-to-all | bytes 65536 | tf_op jit(solution)/shard_map/all_to_all | solution.py:40
  503.0 7.2 %all-to-all-start.6 = ((f32[16,1,512]{2,1,0:T(1,128)}), f32[16,1,512]{2,1,0:T(1,128)S(1)}, u32[]{:S(2)}, u32[]{:S(2)}) async-start(f32[16,1,512]{2,1,0:T(1,128)} %broadcast_in_dim.63), calls=%async_computation.7 | async-start | bytes 65536 | tf_op jit(solution)/shard_map/all_to_all | solution.py:40
  510.3 5.4 fusion.6
  515.7 1.9 copy.87
  517.5 5.8 %all-to-all-start.5 = ((bf16[16,128,512]{1,2,0:T(8,128)(2,1)}), bf16[16,128,512]{1,2,0:T(8,128)(2,1)S(1)}, u32[]{:S(2)}, u32[]{:S(2)}) async-start(bf16[16,128,512]{1,2,0:T(8,128)(2,1)} %bitcast.40), calls=%async_computation.6 | async-start | bytes 4194304 | tf_op jit(solution)/shard_map/all_to_all | solution.py:73
  523.9 27.7 %all-to-all-done.5 = bf16[16,128,512]{1,2,0:T(8,128)(2,1)S(1)} async-done(((bf16[16,128,512]{1,2,0:T(8,128)(2,1)}), bf16[16,128,512]{1,2,0:T(8,128)(2,1)S(1)}, u32[]{:S(2)}, u32[]{:S(2)}) %all-to-all-start.5) | async-done | bytes 2097184 | tf_op jit(solution)/shard_map/all_to_all | solution.py:73
  (60 shorter events, 7.2 us)
Async XLA Ops:
  7.2 2.2 copy-start.4
  7.2 123.6 %all-gather.8.cloned.1.call-start = ((), (), s32[]{:S(2)}) async-start(), calls=%async_computation.10 | async-start | bytes 9437184 | tf_op jit(solution)/shard_map/all_gather | solution.py:95
  7.9 3.3 copy-start
  7.9 222.4 %all-gather.6.cloned.1.call-start = ((), (), s32[]{:S(2)}) async-start(), calls=%async_computation.9 | async-start | bytes 17825792 | tf_op jit(solution)/shard_map/all_gather | solution.py:30
  10.5 353.9 %all-gather.4.cloned.1.call-start = ((), (), s32[]{:S(2)}) async-start(), calls=%async_computation.8 | async-start | bytes 2228224 | tf_op jit(solution)/shard_map/all_gather | solution.py:133
  11.3 2.6 copy-start.7
  246.4 26.3 %all-to-all-start.2 = ((f32[8,1,1024]{2,1,0:T(1,128)}), f32[8,1,1024]{2,1,0:T(1,128)S(1)}, u32[]{:S(2)}, u32[]{:S(2)}) async-start(f32[8,1,1024]{2,1,0:T(1,128)} %broadcast_in_dim.34), calls=%async_computation.2 | async-start | bytes 65536 | tf_op jit(solution)/shard_map/all_to_all | solution.py:40
  252.7 203.5 %reduce-scatter.2.cloned.1.call-start = ((), (), s32[]{:S(2)}) async-start(), calls=%async_computation.11 | async-start | bytes 9437184 | tf_op jit(solution)/shard_map/reduce_scatter | solution.py:115
  260.5 12.2 %copy-start.1 = (bf16[1024,1024]{0,1:T(8,128)(2,1)S(1)}, bf16[1024,1024]{0,1:T(8,128)(2,1)}, u32[]{:S(2)}) copy-start(bf16[1024,1024]{0,1:T(8,128)(2,1)} %copy.67) | copy-start | bytes 6291460
  288.1 1.0 copy-start.3
  291.8 6.7 %copy-start.5 = (s32[16384]{0:T(1024)S(1)}, s32[16384]{0:T(1024)}, u32[]{:S(2)}) copy-start(s32[16384]{0:T(1024)} %param.21) | copy-start | bytes 196612
  291.8 6.9 %copy-start.6 = (s32[1024]{0:T(1024)S(1)}, s32[1024]{0:T(1024)}, u32[]{:S(2)}) copy-start(s32[1024]{0:T(1024)} %param.20) | copy-start | bytes 12292
  291.8 72.6 %all-to-all-start = ((bf16[8,1024,256]{1,2,0:T(8,128)(2,1)}), bf16[8,1024,256]{1,2,0:T(8,128)(2,1)}, u32[]{:S(2)}, u32[]{:S(2)}) async-start(bf16[8,1024,256]{1,2,0:T(8,128)(2,1)} %stack.2), calls=%async_computation | async-start | bytes 8388608 | tf_op jit(solution)/shard_map/all_to_all | solution.py:20
  298.8 7.1 %copy-start.2 = (bf16[1024,512]{1,0:T(8,128)(2,1)S(1)}, bf16[1024,512]{1,0:T(8,128)(2,1)}, u32[]{:S(2)}) copy-start(bf16[1024,512]{1,0:T(8,128)(2,1)} %param.16) | copy-start | bytes 3145732
  371.6 91.4 %all-to-all-start.1 = ((f32[8,1,1024]{2,1,0:T(1,128)}), f32[8,1,1024]{2,1,0:T(1,128)S(1)}, u32[]{:S(2)}, u32[]{:S(2)}) async-start(f32[8,1,1024]{2,1,0:T(1,128)} %broadcast_in_dim.32), calls=%async_computation.1 | async-start | bytes 65536 | tf_op jit(solution)/shard_map/all_to_all | solution.py:40
  461.8 7.1 %copy-start.8 = (bf16[512]{0:T(512)(128)(2,1)S(1)}, bf16[512]{0:T(512)(128)(2,1)}, u32[]{:S(2)}) copy-start(bf16[512]{0:T(512)(128)(2,1)} %param.19) | copy-start | bytes 3076
  463.0 22.8 %all-to-all-start.3 = ((bf16[16,64,513]{2,1,0:T(8,128)(2,1)}), bf16[16,64,513]{2,1,0:T(8,128)(2,1)S(1)}, u32[]{:S(2)}, u32[]{:S(2)}) async-start(bf16[16,64,513]{2,1,0:T(8,128)(2,1)} %pad_maximum_fusion), calls=%async_computation.4 | async-start | bytes 2621440 | tf_op jit(solution)/shard_map/all_to_all | solution.py:54
  503.0 14.5 %all-to-all-start.6 = ((f32[16,1,512]{2,1,0:T(1,128)}), f32[16,1,512]{2,1,0:T(1,128)S(1)}, u32[]{:S(2)}, u32[]{:S(2)}) async-start(f32[16,1,512]{2,1,0:T(1,128)} %broadcast_in_dim.63), calls=%async_computation.7 | async-start | bytes 65536 | tf_op jit(solution)/shard_map/all_to_all | solution.py:40
  517.5 34.1 %all-to-all-start.5 = ((bf16[16,128,512]{1,2,0:T(8,128)(2,1)}), bf16[16,128,512]{1,2,0:T(8,128)(2,1)S(1)}, u32[]{:S(2)}, u32[]{:S(2)}) async-start(bf16[16,128,512]{1,2,0:T(8,128)(2,1)} %bitcast.40), calls=%async_computation.6 | async-start | bytes 4194304 | tf_op jit(solution)/shard_map/all_to_all | solution.py:73
Sparse Core Ops, SparseCore 0:
  10.2 120.5 all-gather.7
  132.4 97.8 all-gather.5
  232.0 33.8 all-gather.3
  288.3 167.8 reduce-scatter.1
